TPU v7x, 512 devices: a whole 4x8x8 slice. The times are simulated.
512 devices in a mesh: shot: 8 (over z), mp: 64 (over x, y, core).
Axes of the slice: x: 4, y: 8, z: 8, core: 2. Of those that a mesh axis runs over, the one named last changes fastest.
Arguments:
- gradient_parts: float32 [32, 4096, 1024], P('shot', 'mp')
- history_s: bfloat16 [10, 4096, 1024], P(None, 'mp'), may hold values from -6 to 6
- history_y: bfloat16 [10, 4096, 1024], P(None, 'mp'), as said below
Outputs:
- direction: float32 [4096, 1024], P('mp', 'shot')
Inputs may be any that keep to these rules, and one draw needn't show every extreme that they name: In every cell, history_y[i] equals history_s[i] times a factor between 0.5 and 4.
All inputs are finite; a program needn't handle non-finite values.
Results may differ from a plain program's by a relative error of at most 0.0003.
Values sent between devices are 32-bit elements; how exact they have to be, the bound alone decides.
A program may use at most 64 MiB of HBM per device.

v0:
```python
import jax
import jax.numpy as jnp
from jax import lax
from jax.sharding import Mesh
from jax.sharding import PartitionSpec as P

M = 10
MP = ("mp_0", "mp_1", "mp_2")


def from_everyone(x, axis):
    copies = jnp.broadcast_to(x, (lax.axis_size(axis), *x.shape))
    return lax.all_to_all(copies, axis, split_axis=0, concat_axis=0, tiled=True)


def taken_together(x, axis):
    everything = from_everyone(x, axis)
    return jnp.sum(everything, axis=0)


def by_axis(x, axes):
    far, near = axes
    return taken_together(taken_together(x, near), far)


def in_blocks(x, dim, length):
    before, after = (x.shape[:dim], x.shape[dim + 1 :])
    return jnp.moveaxis(x.reshape(*before, length, -1, *after), dim, 0)


def sum_at_owner(x, axis, dim):
    blocks = in_blocks(x, dim, lax.axis_size(axis))
    arrived = lax.all_to_all(blocks, axis, split_axis=0, concat_axis=0, tiled=True)
    return arrived.sum(axis=0)


def from_gram(gradient, steps, changes):
    shape = gradient.shape
    flat_grad = gradient.reshape(-1)
    stacked = jnp.concatenate([steps.reshape(M, -1), changes.reshape(M, -1)], axis=0)
    hist_gram = lax.dot_general(
        stacked, stacked, (((1,), (1,)), ((), ())), preferred_element_type=jnp.float32
    )
    stacked_wide = stacked.astype(jnp.float32)
    cross = jnp.dot(stacked_wide, flat_grad, precision=lax.Precision.HIGHEST)
    grad_sq = jnp.sum(flat_grad * flat_grad)
    top = jnp.concatenate([hist_gram, cross[:, None]], axis=1)
    bottom = jnp.concatenate([cross, grad_sq[None]])[None, :]
    gram = by_axis(jnp.concatenate([top, bottom], axis=0), ("shot", ("mp_0", "mp_1", "mp_2")))
    coeffs = jnp.zeros((2 * M + 1,), jnp.float32).at[2 * M].set(1.0)
    alphas = [None] * M
    for i in reversed(range(M)):
        rho_i = 1.0 / gram[i, M + i]
        alphas[i] = rho_i * jnp.dot(gram[i], coeffs, precision=lax.Precision.HIGHEST)
        coeffs = coeffs.at[M + i].add(-alphas[i])
    coeffs = coeffs * (gram[M - 1, 2 * M - 1] / gram[2 * M - 1, 2 * M - 1])
    for i in range(M):
        rho_i = 1.0 / gram[i, M + i]
        beta = rho_i * jnp.dot(gram[M + i], coeffs, precision=lax.Precision.HIGHEST)
        coeffs = coeffs.at[i].add(alphas[i] - beta)
    combined = (
        jnp.dot(coeffs[: 2 * M], stacked_wide, precision=lax.Precision.HIGHEST)
        + coeffs[2 * M] * flat_grad
    )
    return -combined.reshape(shape)


def shards(gradient_parts, history_s, history_y):
    partial_grad = jnp.sum(gradient_parts, axis=0)
    columns = partial_grad.shape[1] // lax.axis_size("shot")
    start = lax.axis_index("shot") * columns
    gradient = sum_at_owner(partial_grad, "shot", 1)
    steps = lax.dynamic_slice_in_dim(history_s, start, columns, 2)
    changes = lax.dynamic_slice_in_dim(history_y, start, columns, 2)
    result = from_gram(gradient, steps, changes)
    return result


def solution(mesh):
    torus = Mesh(
        mesh.devices.reshape(mesh.shape["shot"], 4, 8, 2), ("shot", "mp_0", "mp_1", "mp_2")
    )
    return jax.shard_map(
        shards,
        mesh=torus,
        in_specs=(P("shot", MP, None), P(None, MP, None), P(None, MP, None)),
        out_specs=P(MP, "shot"),
        check_vma=False,
    )
```

profile of v0, /device:TPU:1, one launch (start us, length us, event | category | flops | bytes accessed | tf_op | source)
XLA Modules:
  0.0 114.7 jit_solution(1936361274403318097)
XLA Ops:
  0.0 1.3 %reduce_sum.45 = f32[64,1024]{1,0:T(8,128)S(1)} reduce(f32[4,64,1024]{2,1,0:T(8,128)} %param.45, f32[]{:T(128)} %constant.493.clone.1), dimensions={0}, to_apply=%region_0.0 | reduce | flops 196608 | bytes 1310724 | tf_op jit(solution)/shard_map/reduce_sum | solution.py:69
  2.1 10.9 %all-to-all-start = ((f32[8,64,128]{2,1,0:T(8,128)}), f32[8,64,128]{2,1,0:T(8,128)S(1)}, u32[]{:S(2)}, u32[]{:S(2)}) async-start(f32[8,64,128]{2,1,0:T(8,128)} %copy.14), calls=%async_computation | async-start | bytes 524288 | tf_op jit(solution)/shard_map/all_to_all | solution.py:33
  14.7 8.7 %all-to-all-done = f32[8,64,128]{2,1,0:T(8,128)S(1)} async-done(((f32[8,64,128]{2,1,0:T(8,128)}), f32[8,64,128]{2,1,0:T(8,128)S(1)}, u32[]{:S(2)}, u32[]{:S(2)}) %all-to-all-start) | async-done | bytes 262176 | tf_op jit(solution)/shard_map/all_to_all | solution.py:33
  26.5 22.6 %all_to_all.15 = f32[64,1,441]{2,1,0:T(1,128)S(1)} all-to-all(f32[64,1,441]{2,1,0:T(1,128)S(1)} %reshape.584), channel_id=1, replica_groups=mesh['shot'=8,'mp_0'=4,'mp_1'=8,'mp_2'=2] {'mp_0','mp_1','mp_2'}, dimensions={0} | all-to-all | bytes 225792 | tf_op jit(solution)/shard_map/all_to_all | solution.py:13
  51.9 3.3 %all-to-all-start.2 = ((f32[8,1,441]{2,1,0:T(1,128)}), f32[8,1,441]{2,1,0:T(1,128)S(1)}, u32[]{:S(2)}, u32[]{:S(2)}) async-start(f32[8,1,441]{2,1,0:T(1,128)} %reshape.586), calls=%async_computation.2 | async-start | bytes 32768 | tf_op jit(solution)/shard_map/all_to_all | solution.py:13
  55.2 6.5 %all-to-all-done.2 = f32[8,1,441]{2,1,0:T(1,128)S(1)} async-done(((f32[8,1,441]{2,1,0:T(1,128)}), f32[8,1,441]{2,1,0:T(1,128)S(1)}, u32[]{:S(2)}, u32[]{:S(2)}) %all-to-all-start.2) | async-done | bytes 14144 | tf_op jit(solution)/shard_map/all_to_all | solution.py:13
  65.1 1.3 %fusion.40 = f32[]{:T(128)} fusion(f32[21]{0:T(128)S(1)} %constant_dynamic-update-slice_fusion.19, f32[21,21]{1,0:T(8,128)} %copy-done), kind=kLoop, calls=%fused_computation.66 | loop fusion | flops 41 | bytes 172 | tf_op jit(solution)/shard_map/dot_general | solution.py:54
  67.9 1.3 %fusion.38 = f32[]{:T(128)} fusion(f32[21]{0:T(128)S(1)} %constant_dynamic-update-slice_fusion.18, f32[21,21]{1,0:T(8,128)} %copy-done), kind=kLoop, calls=%fused_computation.63 | loop fusion | flops 41 | bytes 172 | tf_op jit(solution)/shard_map/dot_general | solution.py:54
  70.7 1.3 %fusion.36 = f32[]{:T(128)} fusion(f32[21]{0:T(128)S(1)} %constant_dynamic-update-slice_fusion.17, f32[21,21]{1,0:T(8,128)} %copy-done), kind=kLoop, calls=%fused_computation.60 | loop fusion | flops 41 | bytes 172 | tf_op jit(solution)/shard_map/dot_general | solution.py:54
  73.4 1.3 %fusion.34 = f32[]{:T(128)} fusion(f32[21]{0:T(128)S(1)} %constant_dynamic-update-slice_fusion.16, f32[21,21]{1,0:T(8,128)} %copy-done), kind=kLoop, calls=%fused_computation.57 | loop fusion | flops 41 | bytes 172 | tf_op jit(solution)/shard_map/dot_general | solution.py:54
  76.2 1.3 %fusion.32 = f32[]{:T(128)} fusion(f32[21]{0:T(128)S(1)} %constant_dynamic-update-slice_fusion.15, f32[21,21]{1,0:T(8,128)} %copy-done), kind=kLoop, calls=%fused_computation.54 | loop fusion | flops 41 | bytes 172 | tf_op jit(solution)/shard_map/dot_general | solution.py:54
  78.9 1.3 %fusion.30 = f32[]{:T(128)} fusion(f32[21]{0:T(128)S(1)} %constant_dynamic-update-slice_fusion.14, f32[21,21]{1,0:T(8,128)} %copy-done), kind=kLoop, calls=%fused_computation.51 | loop fusion | flops 41 | bytes 172 | tf_op jit(solution)/shard_map/dot_general | solution.py:54
  81.7 1.3 %fusion.28 = f32[]{:T(128)} fusion(f32[21]{0:T(128)S(1)} %constant_dynamic-update-slice_fusion.13, f32[21,21]{1,0:T(8,128)} %copy-done), kind=kLoop, calls=%fused_computation.48 | loop fusion | flops 41 | bytes 172 | tf_op jit(solution)/shard_map/dot_general | solution.py:54
  84.5 1.3 %fusion.26 = f32[]{:T(128)} fusion(f32[21]{0:T(128)S(1)} %constant_dynamic-update-slice_fusion.12, f32[21,21]{1,0:T(8,128)} %copy-done), kind=kLoop, calls=%fused_computation.45 | loop fusion | flops 41 | bytes 172 | tf_op jit(solution)/shard_map/dot_general | solution.py:54
  87.3 1.3 %fusion.24 = f32[]{:T(128)} fusion(f32[21]{0:T(128)S(1)} %constant_dynamic-update-slice_fusion.11, f32[21,21]{1,0:T(8,128)} %copy-done), kind=kLoop, calls=%fused_computation.42 | loop fusion | flops 41 | bytes 172 | tf_op jit(solution)/shard_map/dot_general | solution.py:54
  91.4 1.3 %fusion.22 = (f32[]{:T(128)}, f32[21]{0:T(128)S(1)}) fusion(f32[21,21]{1,0:T(8,128)} %copy-done, f32[21]{0:T(128)S(1)} %constant_dynamic-update-slice_fusion.10, f32[]{:T(128)} %bitcast.37), kind=kLoop, calls=%fused_computation.39 | loop fusion | flops 62 | bytes 260 | tf_op jit(solution)/shard_map/dot_general | solution.py:59
  93.3 1.4 %fusion.20 = f32[]{:T(128)} fusion(f32[21]{0:T(128)S(1)} %constant_dynamic-update-slice_fusion, f32[21,21]{1,0:T(8,128)} %copy-done), kind=kLoop, calls=%fused_computation.36 | loop fusion | flops 41 | bytes 172 | tf_op jit(solution)/shard_map/dot_general | solution.py:59
  95.5 1.4 %fusion.18 = f32[]{:T(128)} fusion(f32[21]{0:T(128)S(1)} %constant_dynamic-update-slice_fusion.9, f32[21,21]{1,0:T(8,128)} %copy-done), kind=kLoop, calls=%fused_computation.33 | loop fusion | flops 41 | bytes 172 | tf_op jit(solution)/shard_map/dot_general | solution.py:59
  97.7 1.3 %fusion.16 = f32[]{:T(128)} fusion(f32[21]{0:T(128)S(1)} %constant_dynamic-update-slice_fusion.8, f32[21,21]{1,0:T(8,128)} %copy-done), kind=kLoop, calls=%fused_computation.30 | loop fusion | flops 41 | bytes 172 | tf_op jit(solution)/shard_map/dot_general | solution.py:59
  99.8 1.3 %fusion.14 = f32[]{:T(128)} fusion(f32[21]{0:T(128)S(1)} %constant_dynamic-update-slice_fusion.7, f32[21,21]{1,0:T(8,128)} %copy-done), kind=kLoop, calls=%fused_computation.27 | loop fusion | flops 41 | bytes 172 | tf_op jit(solution)/shard_map/dot_general | solution.py:59
  104.0 1.3 %fusion.10 = f32[]{:T(128)} fusion(f32[21]{0:T(128)S(1)} %constant_dynamic-update-slice_fusion.5, f32[21,21]{1,0:T(8,128)} %copy-done), kind=kLoop, calls=%fused_computation.21 | loop fusion | flops 41 | bytes 172 | tf_op jit(solution)/shard_map/dot_general | solution.py:59
  106.1 1.4 %fusion.8 = f32[]{:T(128)} fusion(f32[21]{0:T(128)S(1)} %constant_dynamic-update-slice_fusion.4, f32[21,21]{1,0:T(8,128)} %copy-done), kind=kLoop, calls=%fused_computation.18 | loop fusion | flops 41 | bytes 172 | tf_op jit(solution)/shard_map/dot_general | solution.py:59
  108.2 1.3 %fusion.6 = f32[]{:T(128)} fusion(f32[21]{0:T(128)S(1)} %constant_dynamic-update-slice_fusion.3, f32[21,21]{1,0:T(8,128)} %copy-done), kind=kLoop, calls=%fused_computation.15 | loop fusion | flops 41 | bytes 172 | tf_op jit(solution)/shard_map/dot_general | solution.py:59
  113.4 1.3 %fusion.2 = f32[64,128]{1,0:T(8,128)} fusion(f32[8192]{0:T(1024)S(1)} %bitcast.195, f32[64,128]{1,0:T(8,128)S(1)} %reduce_sum.46, f32[]{:T(128)} %bitcast.60), kind=kLoop, calls=%fused_computation.4 | loop fusion | flops 24576 | bytes 98308 | tf_op jit(solution)/shard_map/neg | solution.py:65
  (57 shorter events, 16.8 us)
Async XLA Ops:
  2.1 21.4 %all-to-all-start = ((f32[8,64,128]{2,1,0:T(8,128)}), f32[8,64,128]{2,1,0:T(8,128)S(1)}, u32[]{:S(2)}, u32[]{:S(2)}) async-start(f32[8,64,128]{2,1,0:T(8,128)} %copy.14), calls=%async_computation | async-start | bytes 524288 | tf_op jit(solution)/shard_map/all_to_all | solution.py:33
  26.5 28.7 %copy-start.1 = (f32[21]{0:T(128)S(1)}, f32[21]{0:T(128)}, u32[]{:S(2)}) copy-start(f32[21]{0:T(128)} %constant.486.clone.1) | copy-start | bytes 256
  51.9 9.9 %all-to-all-start.2 = ((f32[8,1,441]{2,1,0:T(1,128)}), f32[8,1,441]{2,1,0:T(1,128)S(1)}, u32[]{:S(2)}, u32[]{:S(2)}) async-start(f32[8,1,441]{2,1,0:T(1,128)} %reshape.586), calls=%async_computation.2 | async-start | bytes 32768 | tf_op jit(solution)/shard_map/all_to_all | solution.py:13
  62.6 2.5 %copy-start = (f32[21,21]{1,0:T(8,128)}, f32[21,21]{1,0:T(8,128)S(1)}, u32[]{:S(2)}) copy-start(f32[21,21]{1,0:T(8,128)S(1)} %reduce_sum.49) | copy-start | bytes 5296
where the time goes:
time: 116 us; the launch traced here: 115 us
  other arithmetic  34.3 us (30%)
  blocking collectives  22.6 us (19%)
  between operations  20.7 us (18%)
  waiting for transfers between devices  15.3 us (13%)
  starting transfers between devices  14.2 us (12%)
  local copies, waits for them, and re-layouts  6.42 us (6%)
  matrix products  1.2 us (1%)
    all_to_all x1, blocking collectives, from_everyone(): return lax.all_to_all(copies, axis, split_axis=0, concat_axis=0, tiled=True)  22.6 us
    dot_general x10, other arithmetic, from_gram(): beta = rho_i * jnp.dot(gram[M + i], coeffs, precision=lax.Precision.HIGHEST)  13.2 us
    dot_general x10, other arithmetic, from_gram(): jnp.dot(gram[i], coeffs, precision=lax.Precision.HIGHEST)  12.4 us
    all_to_all x1, starting transfers between devices, sum_at_owner(): lax.all_to_all(blocks, axis, split_axis=0, concat_axis=0, tiled=True)  10.9 us
    all_to_all x1, waiting for transfers between devices, sum_at_owner(): lax.all_to_all(blocks, axis, split_axis=0, concat_axis=0, tiled=True)  8.74 us
    all_to_all x1, waiting for transfers between devices, from_everyone(): return lax.all_to_all(copies, axis, split_axis=0, concat_axis=0, tiled=True)  6.54 us
    all_to_all x1, starting transfers between devices, from_everyone(): return lax.all_to_all(copies, axis, split_axis=0, concat_axis=0, tiled=True)  3.34 us
    unnamed x14, local copies, waits for them, and re-layouts  2.44 us
  transfers between devices with their start and end apart: 2, of which 2 were waited for; matrix products, arithmetic and copies ran while one was open for 2% of the time, Pallas kernels for 0%

commit v1 on v0

v1 whole, which is shorter than its diff:
```python
import functools

import jax
import jax.numpy as jnp
from jax import lax
from jax.experimental import pallas as pl
from jax.experimental.pallas import tpu as pltpu
from jax.sharding import Mesh
from jax.sharding import PartitionSpec as P

M = 10
MP = ("mp_0", "mp_1", "mp_2")
MESH = pl.DeviceIdType.MESH
CHUNK = 16
GROUP = 72
PAIRS = [(i, j) for i in range(M) for j in range(i, M)]
ROW = {pair: k for k, pair in enumerate(PAIRS)}
CROSS = len(PAIRS)


def folded(x):
    rows = x.shape[0]
    parts = [x[8 * t : 8 * t + 8] for t in range(rows // 8)]
    while len(parts) > 1:
        parts = [a + b for a, b in zip(parts[::2], parts[1::2])]
    return parts[0]


def kernel(
    sizes,
    parts_hbm,
    s_hbm,
    y_hbm,
    out_ref,
    parts_v,
    s_v,
    y_v,
    part_v,
    got_v,
    mine_v,
    acc_v,
    wide_v,
    msg_v,
    in_v,
    load_sem,
    g_send,
    g_recv,
    m_send,
    m_recv,
):
    nz, nx, ny, nc = sizes
    z, x, y, c = (lax.axis_index(name) for name in ("shot", *MP))
    rows = s_v.shape[1]
    width = s_v.shape[2]
    cols = width // nz
    chunks = rows // CHUNK

    def load(k, src, dst, which):
        span = pl.ds(k * CHUNK, CHUNK)
        return pltpu.make_async_copy(
            src.at[:, span, :], dst.at[:, span, :], load_sem.at[which, k]
        )

    for k in range(chunks):
        load(k, parts_hbm, parts_v, 0).start()
    for k in range(chunks):
        load(k, s_hbm, s_v, 1).start()
        load(k, y_hbm, y_v, 2).start()

    stages = (
        [
            {"mp_0": lax.rem(x + dx, nx), "mp_2": lax.rem(c + dc, nc)}
            for dx in range(nx)
            for dc in range(nc)
            if dx + dc
        ],
        [{"mp_1": lax.rem(y + d, ny)} for d in range(1, ny)],
        [{"shot": lax.rem(z + d, nz)} for d in range(1, nz)],
    )

    def device(where):
        here = {"shot": z, "mp_0": x, "mp_1": y, "mp_2": c}
        here.update(where)
        return (here["shot"], here["mp_0"], here["mp_1"], here["mp_2"])

    barrier = pltpu.get_barrier_semaphore()
    for stage in stages:
        for where in stage:
            pl.semaphore_signal(
                barrier, inc=1, device_id=device(where), device_id_type=MESH
            )

    for k in range(chunks):
        load(k, parts_hbm, parts_v, 0).wait()
        span = pl.ds(k * CHUNK, CHUNK)
        total = parts_v[0, span, :]
        for shot in range(1, parts_v.shape[0]):
            total = total + parts_v[shot, span, :]
        for block in range(nz):
            part_v[block, span, :] = total[:, block * cols : (block + 1) * cols]

    def cross(k, sums):
        load(k, s_hbm, s_v, 1).wait()
        load(k, y_hbm, y_v, 2).wait()
        span = pl.ds(pl.multiple_of(k * CHUNK, CHUNK), CHUNK)
        grads = [part_v[block, span, :] for block in range(nz)]
        new = []
        for n, acc in enumerate(sums):
            vec = s_v if n < M else y_v
            values = vec[n % M, span, :].astype(jnp.float32)
            prods = [
                values[:, block * cols : (block + 1) * cols] * grads[block]
                for block in range(nz)
            ]
            while len(prods) > 1:
                prods = [a + b for a, b in zip(prods[::2], prods[1::2])]
            new.append(acc + folded(prods[0]))
        return tuple(new)

    zero = jnp.zeros((8, cols), jnp.float32)
    sums = lax.fori_loop(0, chunks, cross, (zero,) * (2 * M))
    for n in range(2 * M):
        at = (n // M) * GROUP + CROSS + n % M
        acc_v[8 * at : 8 * at + 8, :] = sums[n]
    for group in range(2):
        for at in range(group * GROUP + CROSS + M, (group + 1) * GROUP):
            acc_v[8 * at : 8 * at + 8, :] = zero

    own = pl.ds(pl.multiple_of(z * cols, cols), cols)
    for n in range(M):
        mine_v[n] = s_v[n, :, own].astype(jnp.float32)
        mine_v[M + n] = y_v[n, :, own].astype(jnp.float32)
    for (i, j), at in ROW.items():
        right = mine_v[M + j]
        acc_v[8 * at : 8 * at + 8, :] = folded(mine_v[i] * right)
        at = at + GROUP
        acc_v[8 * at : 8 * at + 8, :] = folded(mine_v[M + i] * right)

    slabs = [acc_v[pl.ds(r, 2 * GROUP, stride=8), :] for r in range(8)]
    while len(slabs) > 1:
        slabs = [a + b for a, b in zip(slabs[::2], slabs[1::2])]
    lanes = jnp.sum(slabs[0], axis=1, keepdims=True)
    eye = lax.broadcasted_iota(jnp.int32, (GROUP, cols), 0) == lax.broadcasted_iota(
        jnp.int32, (GROUP, cols), 1
    )
    for group in range(2):
        column = lanes[group * GROUP : (group + 1) * GROUP]
        line = jnp.where(eye, jnp.broadcast_to(column, (GROUP, cols)), 0.0)
        msg_v[0, group : group + 1, :] = jnp.sum(line, axis=0, keepdims=True)

    pl.semaphore_wait(barrier, sum(len(stage) for stage in stages))

    def share(n, d):
        return pltpu.make_async_remote_copy(
            src_ref=msg_v.at[n],
            dst_ref=in_v.at[n, d],
            send_sem=m_send.at[n, d],
            recv_sem=m_recv.at[n, d],
            device_id=device(stages[n][d]),
            device_id_type=MESH,
        )

    def give(d):
        return pltpu.make_async_remote_copy(
            src_ref=part_v.at[lax.rem(z + d + 1, nz)],
            dst_ref=got_v.at[d],
            send_sem=g_send.at[d],
            recv_sem=g_recv.at[d],
            device_id=device(stages[2][d]),
            device_id_type=MESH,
        )

    for d in range(len(stages[0])):
        share(0, d).start()
    for d in range(nz - 1):
        give(d).start()

    for n in range(3):
        count = len(stages[n])
        if n == 2:
            grad = part_v[z]
            for d in range(nz - 1):
                give(d).wait_recv()
                grad = grad + got_v[d]
        total = msg_v[n]
        for d in range(count):
            share(n, d).wait_recv()
            total = total + in_v[n, d]
        if n < 2:
            msg_v[n + 1] = total
            for d in range(len(stages[n + 1])):
                share(n + 1, d).start()

    for group in range(2):
        line = jnp.broadcast_to(total[group : group + 1], (GROUP, cols))
        column = jnp.sum(jnp.where(eye, line, 0.0), axis=1, keepdims=True)
        wide_v[group * GROUP : (group + 1) * GROUP, :] = jnp.broadcast_to(
            column, (GROUP, cols)
        )

    def splat(at):
        return jnp.broadcast_to(wide_v[at : at + 1, :], (8, cols))

    sy = {pair: splat(at) for pair, at in ROW.items()}
    yy = {pair: splat(GROUP + at) for pair, at in ROW.items()}
    sg = [splat(CROSS + i) for i in range(M)]
    yg = [splat(GROUP + CROSS + i) for i in range(M)]
    rho = [1.0 / sy[i, i] for i in range(M)]
    gamma = sy[M - 1, M - 1] / yy[M - 1, M - 1]
    alpha = [None] * M
    for i in reversed(range(M)):
        alpha[i] = rho[i] * sg[i]
        for j in range(i):
            sg[j] = sg[j] - alpha[i] * sy[j, i]
        for j in range(M):
            yg[j] = yg[j] - alpha[i] * yy[min(i, j), max(i, j)]
    yg = [gamma * v for v in yg]
    delta = [None] * M
    for i in range(M):
        delta[i] = alpha[i] - rho[i] * yg[i]
        for j in range(i + 1, M):
            yg[j] = yg[j] + delta[i] * sy[i, j]
    shape = (rows // 8, 8, cols)
    back = grad.reshape(shape)
    for i in range(M):
        back = back - alpha[i][None] * mine_v[M + i].reshape(shape)
    back = gamma[None] * back
    for i in range(M):
        back = back + delta[i][None] * mine_v[i].reshape(shape)
    out_ref[...] = -back.reshape(rows, cols)

    for n in range(3):
        for d in range(len(stages[n])):
            share(n, d).wait_send()
    for d in range(nz - 1):
        give(d).wait_send()


def solution(mesh):
    nz, ny, nc = mesh.shape["shot"], 8, 2
    nx = mesh.shape["mp"] // (ny * nc)
    torus = Mesh(mesh.devices.reshape(nz, nx, ny, nc), ("shot", *MP))

    def shards(gradient_parts, history_s, history_y):
        shots, rows, width = gradient_parts.shape
        cols = width // nz
        f32, bf16 = jnp.float32, jnp.bfloat16
        most = max(nx * nc, ny, nz) - 1
        return pl.pallas_call(
            functools.partial(kernel, (nz, nx, ny, nc)),
            out_shape=jax.ShapeDtypeStruct((rows, cols), f32),
            in_specs=[pl.BlockSpec(memory_space=pl.ANY)] * 3,
            out_specs=pl.BlockSpec(memory_space=pltpu.VMEM),
            scratch_shapes=[
                pltpu.VMEM((shots, rows, width), f32),
                pltpu.VMEM((M, rows, width), bf16),
                pltpu.VMEM((M, rows, width), bf16),
                pltpu.VMEM((nz, rows, cols), f32),
                pltpu.VMEM((nz - 1, rows, cols), f32),
                pltpu.VMEM((2 * M, rows, cols), f32),
                pltpu.VMEM((2 * GROUP * 8, cols), f32),
                pltpu.VMEM((2 * GROUP, cols), f32),
                pltpu.VMEM((3, 2, cols), f32),
                pltpu.VMEM((3, most, 2, cols), f32),
                pltpu.SemaphoreType.DMA((3, rows // CHUNK)),
                pltpu.SemaphoreType.DMA((nz - 1,)),
                pltpu.SemaphoreType.DMA((nz - 1,)),
                pltpu.SemaphoreType.DMA((3, most)),
                pltpu.SemaphoreType.DMA((3, most)),
            ],
            compiler_params=pltpu.CompilerParams(collective_id=0, has_side_effects=True),
        )(gradient_parts, history_s, history_y)

    return jax.shard_map(
        shards,
        mesh=torus,
        in_specs=(P("shot", MP, None), P(None, MP, None), P(None, MP, None)),
        out_specs=P(MP, "shot"),
        check_vma=False,
    )
```

time: 116 us -> 29.5 us (0.25)
  other arithmetic: 34.3 us -> 0 us
  Pallas kernels: 0 us -> 27.9 us
  blocking collectives: 22.6 us -> 0 us
  between operations: 20.7 us -> 0.01 us
  waiting for transfers between devices: 15.3 us -> 0 us
  starting transfers between devices: 14.2 us -> 0 us
  local copies, waits for them, and re-layouts: 6.42 us -> 1.38 us
  matrix products: 1.2 us -> 0 us
    pallas_call x0 -> x1, Pallas kernels: none -> 27.9 us  [shards(): pl.pallas_call(functools.partial(kernel, (nz, nx, ny, nc)), out_shape=jax...]
    dot_general x20 -> x0, other arithmetic: 25.7 us -> none  [the longest x10 13.2 us: from_gram(): beta = rho_i * jnp.dot(gram[M + i], coeffs, precision=lax.Precision.HIGHEST)]
    all_to_all x1 -> x0, blocking collectives: 22.6 us -> none  [from_everyone(): return lax.all_to_all(copies, axis, split_axis=0, concat_axis=0, tiled=True)]
    all_to_all x2 -> x0, waiting for transfers between devices: 15.3 us -> none  [the longest x1 8.74 us: sum_at_owner(): lax.all_to_all(blocks, axis, split_axis=0, concat_axis=0, tiled=True)]
    all_to_all x2 -> x0, starting transfers between devices: 14.2 us -> none  [the longest x1 10.9 us: sum_at_owner(): lax.all_to_all(blocks, axis, split_axis=0, concat_axis=0, tiled=True)]
    scatter-add x19 -> x0, other arithmetic: 2.73 us -> none  [the longest x10 1.38 us: from_gram(): coeffs = coeffs.at[i].add(alphas[i] - beta)]
    reduce_sum x5 -> x0, other arithmetic: 2.04 us -> none  [the longest x1 1.31 us: shards(): partial_grad = jnp.sum(gradient_parts, axis=0)]
    all_to_all x2 -> x0, other arithmetic: 1.72 us -> none  [from_everyone(): return lax.all_to_all(copies, axis, split_axis=0, concat_axis=0, tiled=True)]
  transfers between devices with their start and end apart: 2 -> 0, of which waited for: 2 -> 0; matrix products, arithmetic and copies ran while one was open for 2% -> 0% of each run, Pallas kernels for 0% -> 0%
where the time goes in v1:
time: 29.5 us; the launch traced here: 29.3 us
  Pallas kernels  27.9 us (95%)
  local copies, waits for them, and re-layouts  1.38 us (5%)
    pallas_call x1, Pallas kernels, shards(): pl.pallas_call(functools.partial(kernel, (nz, nx, ny, nc)), out_shape=jax...  27.9 us
    unnamed x1, local copies, waits for them, and re-layouts  1.38 us

profile of v1, /device:TPU:1, one launch (start us, length us, event | category | flops | bytes accessed | tf_op | source)
XLA Modules:
  0.0 29.3 jit_solution(1609325691978517156)
XLA Ops:
  0.0 27.9 %shard_map.37 = f32[64,128]{1,0:T(8,128)} custom-call(f32[4,64,1024]{2,1,0:T(8,128)} %parts_hbm.1, bf16[10,64,1024]{2,1,0:T(8,128)(2,1)} %s_hbm.1, bf16[10,64,1024]{2,1,0:T(8,128)(2,1)} %y_hbm.1), custom_call_target="tpu_custom_call" | custom-call | tf_op jit(solution)/shard_map/pallas_call | solution.py:249
  27.9 1.4 %copy.5 = f32[64,128]{1,0:T(8,128)} copy(f32[64,128]{1,0:T(8,128)} %shard_map.37) | data formatting | bytes 65536
